TPU v7x, 32 devices: a whole 2x2x4 slice. The times are simulated.
32 devices in a mesh: rows: 8 (over z, y), grp: 4 (over x, core).
Axes of the slice: x: 2, y: 2, z: 4, core: 2. Of those that a mesh axis runs over, the one named last changes fastest.
Arguments:
- owner: int32 [1024, 24, 3], P('rows', 'grp'), may hold values from 0 to 7, as said below
- offset: int32 [1024, 24, 3], P('rows', 'grp'), may hold values from 0 to 511
- tables: float32 [12, 4096, 128], P('grp', 'rows'), may hold values from -6 to 6
- w_first: bfloat16 [3072, 1024], P('grp'), may hold values from -0.109375 to 0.109375
- b_first: float32 [1024], replicated, may hold values from -3 to 3
- w_out: float32 [1024], replicated, may hold values from -0.1875 to 0.1875
- labels: int32 [1024], P('rows'), may hold values 0 or 1
Outputs:
- table_grad: float32 [12, 4096, 128], P('grp', 'rows')
- losses: float32 [1024], P(('rows', 'grp'))
Inputs may be any that keep to these rules, and one draw needn't show every extreme that they name: Of the lookups of one device (its 128 samples and 6 features, all three hashes) at most 1032 name one owner, and in every draw some owner gets exactly 1032. Among the lookups of one device to one owner for one table, at most 114 distinct offsets occur, and that bound is reached in every draw.
All inputs are finite; a program needn't handle non-finite values. No bound on the sum of `labels` on one device may be relied on, other than what follows from the above.
Results may differ from a plain program's by a relative error of at most 0.005.
Values may be sent and summed in bfloat16 or wider, within the bound.
A program may use at most 64 MiB of HBM per device.

v0:
```python
import jax
import jax.numpy as jnp
from jax import lax
from jax.sharding import PartitionSpec as P


def head_loss(pre_act, w_out, targets):
    gate_sig = jax.nn.sigmoid(pre_act)
    logits = jnp.sum(pre_act * gate_sig * w_out, axis=1)
    losses = jax.nn.softplus(logits) - targets * logits
    grad_logit = jax.nn.sigmoid(logits) - targets
    grad_pre = (
        grad_logit[:, None] * w_out * (gate_sig * (1.0 + pre_act * (1.0 - gate_sig)))
    ).astype(jnp.bfloat16)
    return (losses, grad_pre)


def run_starts(sorted_values, values_index):
    is_first = jnp.concatenate([jnp.ones((1,), bool), sorted_values[1:] != sorted_values[:-1]])
    return lax.cummax(jnp.where(is_first, values_index, 0), axis=0)


def body(owner, offset, tables, w_first, b_first, w_out, labels):
    row_devices = lax.axis_size("rows")
    bdev_rows, fgrp_count = (owner.shape[0], owner.shape[1])
    rows_dev, emb_width = (tables.shape[1], tables.shape[2])
    lookups = bdev_rows * fgrp_count * 3
    hot_count = 8 * (bdev_rows * fgrp_count * 7 // (16 * row_devices)) + 8
    owner_flat = owner.reshape(-1)
    offset_flat = offset.reshape(-1)
    positions = jnp.arange(lookups, dtype=jnp.int32)
    table_kind = positions % 3
    flat_table = tables.reshape(3 * rows_dev, emb_width)
    unique_cap = hot_count // 3
    group_key = (owner_flat * 3 + table_kind) * rows_dev + offset_flat
    ordering = jnp.argsort(group_key, stable=True)
    sorted_keys = group_key[ordering]
    is_new = jnp.concatenate([jnp.ones((1,), bool), sorted_keys[1:] != sorted_keys[:-1]])
    unique_id = jnp.cumsum(is_new.astype(jnp.int32)) - 1
    sorted_group = sorted_keys // rows_dev
    slot_sorted = sorted_group * unique_cap + unique_id - run_starts(sorted_group, unique_id)
    slot_of = jnp.zeros((lookups,), jnp.int32).at[ordering].set(slot_sorted)
    outgoing = jnp.full((row_devices * 3 * unique_cap,), -1, jnp.int32).at[slot_of].set(offset_flat)
    row_codes = lax.all_to_all(
        outgoing.reshape(row_devices, 3, unique_cap),
        "rows",
        split_axis=0,
        concat_axis=0,
        tiled=True,
    )
    is_live = (row_codes >= 0)[..., None]
    row_index = jnp.arange(3, dtype=jnp.int32)[None, :, None] * rows_dev + jnp.maximum(row_codes, 0)
    fetched = jnp.take(flat_table, row_index.reshape(-1), axis=0)
    fetched = (fetched.reshape(row_codes.shape + (emb_width,)) * is_live).astype(jnp.bfloat16)
    returned = lax.all_to_all(fetched, "rows", split_axis=0, concat_axis=0, tiled=True)
    owner_codes, returned = (row_codes, returned)
    owner_index = (
        jnp.arange(3, dtype=jnp.int32)[None, :, None] * rows_dev + jnp.maximum(owner_codes, 0)
    ).reshape(-1)
    looked = (
        returned.reshape(-1, emb_width)[slot_of]
        .astype(jnp.float32)
        .reshape(bdev_rows, fgrp_count, 3, emb_width)
    )
    embedded = looked[:, :, 0] * looked[:, :, 1] + looked[:, :, 2]
    features = embedded.reshape(bdev_rows, fgrp_count * emb_width).astype(jnp.bfloat16)
    targets = labels.astype(jnp.float32)
    share_rows = bdev_rows // lax.axis_size("grp")
    share_start = lax.axis_index("grp") * share_rows
    partial_pre = jnp.dot(features, w_first, preferred_element_type=jnp.float32)
    pre_act = lax.psum(partial_pre, "grp") + b_first
    all_losses, grad_pre = head_loss(pre_act, w_out, targets)
    losses = lax.dynamic_slice_in_dim(all_losses, share_start, share_rows, 0)
    grad_emb = jnp.dot(grad_pre, w_first.T, preferred_element_type=jnp.float32).reshape(
        bdev_rows, fgrp_count, emb_width
    )
    row_grads = jnp.stack(
        [grad_emb * looked[:, :, 1], grad_emb * looked[:, :, 0], grad_emb], axis=2
    ).reshape(lookups, emb_width)
    outgoing_grads = (
        jnp.zeros((row_devices * 3 * unique_cap, emb_width), jnp.float32).at[slot_of].add(row_grads)
    )
    received = lax.all_to_all(
        outgoing_grads.reshape(row_devices, 3, unique_cap, emb_width),
        "rows",
        split_axis=0,
        concat_axis=0,
        tiled=True,
    )
    table_grad = (
        jnp.zeros((3 * rows_dev, emb_width), jnp.float32)
        .at[owner_index]
        .add(received.reshape(-1, emb_width))
    )
    return (table_grad.reshape(3, rows_dev, emb_width), losses)


def solution(mesh):
    placed = (
        P("rows", "grp", None),
        P("rows", "grp", None),
        P("grp", "rows", None),
        P("grp", None),
        P(),
        P(),
        P("rows"),
    )
    return jax.shard_map(
        body,
        mesh=mesh,
        in_specs=placed,
        out_specs=(P("grp", "rows", None), P(("rows", "grp"))),
        check_vma=False,
    )
```

profile of v0, /device:TPU:0, one launch (start us, length us, event | category | flops | bytes accessed | tf_op | source)
XLA Modules:
  0.0 225.8 jit_solution(1120389095388177979)
XLA Ops:
  9.7 5.8 %sort.17 = (s32[2304]{0:T(1024)}, s32[2304]{0:T(1024)S(1)}) sort(s32[2304]{0:T(1024)S(1)} %fusion.12, s32[2304]{0:T(1024)S(1)} %iota.15), dimensions={0}, to_apply=%region_0.1 | sort | flops 27648 | bytes 36864 | tf_op jit(solution)/shard_map/jit(argsort)/sort | solution.py:36
  15.5 12.3 %gather_fusion = s32[2304]{0:T(1024)S(1)} fusion(s32[2304]{0:T(1024)S(1)} %fusion.12, s32[3072]{0:T(1024)S(1)} %pad_clamp_fusion.2), kind=kCustom, calls=%fused_computation | custom fusion | bytes 27648 | tf_op jit(solution)/shard_map/gather | solution.py:37
  29.2 9.0 %scatter_custom_fusion = s32[2304]{0:T(1024)S(1)} fusion(s32[2304]{0:T(1024)S(1)} %compare_select_fusion.3, s32[2304]{0:T(1024)S(1)} %bitcast_subtract_fusion, s32[]{:T(128)} %constant.33.clone.1), kind=kCustom, calls=%fused_computation.64 | custom fusion | bytes 9220 | tf_op jit(solution)/shard_map/scatter | solution.py:42
  38.2 9.0 %scatter_custom_fusion.1 = s32[2736]{0:T(1024)S(1)} fusion(s32[2304]{0:T(1024)S(1)} %compare_select_fusion.2, s32[2304]{0:T(1024)S(1)} %reshape.183, s32[]{:T(128)} %constant.31.clone.1), kind=kCustom, calls=%fused_computation.66 | custom fusion | bytes 10948 | tf_op jit(solution)/shard_map/scatter | solution.py:43
  48.0 7.3 %all-to-all-start = ((s32[8,3,114]{2,1,0:T(4,128)}), s32[8,3,114]{2,1,0:T(4,128)S(1)}, u32[]{:S(2)}, u32[]{:S(2)}) async-start(s32[8,3,114]{2,1,0:T(4,128)} %reshape.136), calls=%async_computation | async-start | bytes 32768 | tf_op jit(solution)/shard_map/all_to_all | solution.py:44
  55.3 6.6 %all-to-all-done = s32[8,3,114]{2,1,0:T(4,128)S(1)} async-done(((s32[8,3,114]{2,1,0:T(4,128)}), s32[8,3,114]{2,1,0:T(4,128)S(1)}, u32[]{:S(2)}, u32[]{:S(2)}) %all-to-all-start) | async-done | bytes 10976 | tf_op jit(solution)/shard_map/all_to_all | solution.py:44
  62.1 5.9 %gather_fusion.1 = f32[2736,128]{1,0:T(8,128)} fusion(f32[1536,128]{1,0:T(8,128)S(1)} %bitcast.21, s32[3072]{0:T(1024)S(1)} %pad_clamp_fusion.1), kind=kCustom, calls=%fused_computation.1 | custom fusion | bytes 2812608 | tf_op jit(solution)/shard_map/jit(_take)/gather | solution.py:53
  68.0 1.4 gather.14
  69.5 2.1 multiply_convert_fusion
  71.5 3.5 %all-to-all-start.1 = ((bf16[8,3,114,128]{3,2,1,0:T(8,128)(2,1)}), bf16[8,3,114,128]{3,2,1,0:T(8,128)(2,1)S(1)}, u32[]{:S(2)}, u32[]{:S(2)}) async-start(bf16[8,3,114,128]{3,2,1,0:T(8,128)(2,1)} %multiply_convert_fusion), calls=%async_computation.1 | async-start | bytes 1474560 | tf_op jit(solution)/shard_map/all_to_all | solution.py:55
  75.3 17.6 %all-to-all-done.1 = bf16[8,3,114,128]{3,2,1,0:T(8,128)(2,1)S(1)} async-done(((bf16[8,3,114,128]{3,2,1,0:T(8,128)(2,1)}), bf16[8,3,114,128]{3,2,1,0:T(8,128)(2,1)S(1)}, u32[]{:S(2)}, u32[]{:S(2)}) %all-to-all-start.1) | async-done | bytes 700448 | tf_op jit(solution)/shard_map/all_to_all | solution.py:55
  93.2 5.6 %gather_fusion.2 = bf16[2304,128]{1,0:T(8,128)(2,1)} fusion(bf16[2736,128]{1,0:T(8,128)(2,1)S(1)} %reshape.139, s32[3072]{0:T(1024)S(1)} %pad_clamp_fusion), kind=kCustom, calls=%fused_computation.2 | custom fusion | bytes 1188864 | tf_op jit(solution)/shard_map/gather | solution.py:61
  98.8 2.0 reshape.146
  102.7 1.2 fusion.28
  103.9 32.6 %all-reduce.2.cloned.1.call-done = f32[128,1024]{1,0:T(8,128)} async-done(((f32[128,1024]{1,0:T(8,128)}), f32[128,1024]{1,0:T(8,128)}) %all-reduce.2.cloned.1.call-update) | async-done | bytes 524304 | tf_op jit(solution)/shard_map/psum | solution.py:71
  136.5 1.3 multiply_reduce_fusion
  137.8 1.8 fusion.5
  140.8 1.4 reshape.191
  142.1 14.9 %scatter_custom_fusion.2 = f32[2736,128]{1,0:T(8,128)S(1)} fusion(s32[2304]{0:T(1024)} %copy-done.4, f32[2304,128]{1,0:T(8,128)} %reshape.191, f32[]{:T(128)} %constant.26.clone.1), kind=kCustom, calls=%fused_computation.9 | custom fusion | flops 294912 | bytes 1401344 | tf_op jit(solution)/shard_map/scatter-add | solution.py:81
  157.1 1.2 reshape.142
  158.3 5.5 %all-to-all-start.2 = ((f32[8,3,114,128]{3,2,1,0:T(8,128)}), f32[8,3,114,128]{3,2,1,0:T(8,128)S(1)}, u32[]{:S(2)}, u32[]{:S(2)}) async-start(f32[8,3,114,128]{3,2,1,0:T(8,128)} %reshape.142), calls=%async_computation.2 | async-start | bytes 2949120 | tf_op jit(solution)/shard_map/all_to_all | solution.py:83
  164.4 33.5 %all-to-all-done.2 = f32[8,3,114,128]{3,2,1,0:T(8,128)S(1)} async-done(((f32[8,3,114,128]{3,2,1,0:T(8,128)}), f32[8,3,114,128]{3,2,1,0:T(8,128)S(1)}, u32[]{:S(2)}, u32[]{:S(2)}) %all-to-all-start.2) | async-done | bytes 1400864 | tf_op jit(solution)/shard_map/all_to_all | solution.py:83
  197.9 1.2 reshape.199
  199.1 19.9 %scatter_custom_fusion.3 = f32[1536,128]{1,0:T(8,128)} fusion(s32[2736]{0:T(1024)S(1)} %fusion.20, f32[2736,128]{1,0:T(8,128)} %reshape.199, f32[]{:T(128)} %constant.26.clone.1), kind=kCustom, calls=%fused_computation.16 | custom fusion | flops 350208 | bytes 786944 | tf_op jit(solution)/shard_map/scatter-add | solution.py:93
  (59 shorter events, 8.9 us)
Async XLA Ops:
  7.2 95.5 %copy-start = (bf16[768,1024]{1,0:T(8,128)(2,1)S(1)}, bf16[768,1024]{1,0:T(8,128)(2,1)}, u32[]{:S(2)}) copy-start(bf16[768,1024]{1,0:T(8,128)(2,1)} %param.10) | copy-start | bytes 4718596
  15.4 46.7 %copy-start.1 = (f32[3,512,128]{2,1,0:T(8,128)S(1)}, f32[3,512,128]{2,1,0:T(8,128)}, u32[]{:S(2)}) copy-start(f32[3,512,128]{2,1,0:T(8,128)} %param.9) | copy-start | bytes 2359300
  38.2 37.1 %copy-start.4 = (s32[2304]{0:T(1024)}, s32[2304]{0:T(1024)S(1)}, u32[]{:S(2)}) copy-start(s32[2304]{0:T(1024)S(1)} %compare_select_fusion.2) | copy-start | bytes 27652
  48.0 13.9 %all-to-all-start = ((s32[8,3,114]{2,1,0:T(4,128)}), s32[8,3,114]{2,1,0:T(4,128)S(1)}, u32[]{:S(2)}, u32[]{:S(2)}) async-start(s32[8,3,114]{2,1,0:T(4,128)} %reshape.136), calls=%async_computation | async-start | bytes 32768 | tf_op jit(solution)/shard_map/all_to_all | solution.py:44
  71.5 21.4 %all-to-all-start.1 = ((bf16[8,3,114,128]{3,2,1,0:T(8,128)(2,1)}), bf16[8,3,114,128]{3,2,1,0:T(8,128)(2,1)S(1)}, u32[]{:S(2)}, u32[]{:S(2)}) async-start(bf16[8,3,114,128]{3,2,1,0:T(8,128)(2,1)} %multiply_convert_fusion), calls=%async_computation.1 | async-start | bytes 1474560 | tf_op jit(solution)/shard_map/all_to_all | solution.py:55
  75.1 61.4 %all-reduce.2.cloned.1.call-start = ((), (), s32[]{:S(2)}) async-start(), calls=%async_computation.3 | async-start | bytes 1048576 | tf_op jit(solution)/shard_map/psum | solution.py:71
  101.6 0.8 copy-start.2
  102.6 33.8 %copy-start.5 = (f32[1024]{0:T(1024)S(1)}, f32[1024]{0:T(1024)}, u32[]{:S(2)}) copy-start(f32[1024]{0:T(1024)} %param.12) | copy-start | bytes 12292
  102.6 33.8 %copy-start.6 = (f32[1024]{0:T(1024)S(1)}, f32[1024]{0:T(1024)}, u32[]{:S(2)}) copy-start(f32[1024]{0:T(1024)} %param.11) | copy-start | bytes 12292
  102.7 35.1 %copy-start.7 = (s32[128]{0:T(128)S(1)}, s32[128]{0:T(128)}, u32[]{:S(2)}) copy-start(s32[128]{0:T(128)} %param.13) | copy-start | bytes 1540
  137.8 2.0 copy-start.3
  158.3 39.6 %all-to-all-start.2 = ((f32[8,3,114,128]{3,2,1,0:T(8,128)}), f32[8,3,114,128]{3,2,1,0:T(8,128)S(1)}, u32[]{:S(2)}, u32[]{:S(2)}) async-start(f32[8,3,114,128]{3,2,1,0:T(8,128)} %reshape.142), calls=%async_computation.2 | async-start | bytes 2949120 | tf_op jit(solution)/shard_map/all_to_all | solution.py:83
Sparse Core Ops, SparseCore 0:
  104.0 32.4 all-reduce.1
where the time goes:
time: 226 us
  waiting for transfers between devices  90.3 us (40%)
  local copies, waits for them, and re-layouts  55.4 us (25%)
  other arithmetic  46.2 us (20%)
  starting transfers between devices  16.6 us (7%)
  between operations  14.3 us (6%)
  matrix products  3 us (1%)
    all_to_all x1, waiting for transfers between devices, body(): lax.all_to_all(outgoing_grads.reshape(row_devices, 3, unique_cap, emb_wid...  33.5 us
    psum x1, waiting for transfers between devices, body(): pre_act = lax.psum(partial_pre, 'grp') + b_first  32.6 us
    scatter-add x1, other arithmetic, body(): table_grad = jnp.zeros((3 * rows_dev, emb_width), jnp.float32).at[owner_i...  19.9 us
    all_to_all x1, waiting for transfers between devices, body(): lax.all_to_all(fetched, 'rows', split_axis=0, concat_axis=0, tiled=True)  17.6 us
    scatter-add x1, other arithmetic, body(): jnp.zeros((row_devices * 3 * unique_cap, emb_width), jnp.float32)  14.9 us
    gather x1, local copies, waits for them, and re-layouts, body(): sorted_keys = group_key[ordering]  12.3 us
    scatter x1, local copies, waits for them, and re-layouts, body(): slot_of = jnp.zeros((lookups,), jnp.int32).at[ordering].set(slot_sorted)  9 us
    scatter x1, local copies, waits for them, and re-layouts, body(): jnp.full((row_devices * 3 * unique_cap,), -1, jnp.int32).at[slot_of]  8.99 us
  transfers between devices with their start and end apart: 4, of which 4 were waited for; matrix products, arithmetic and copies ran while one was open for 0% of the time, Pallas kernels for 0%

commit v1 on v0

v1 whole, which is shorter than its diff:
```python
import functools

import jax
import jax.numpy as jnp
from jax import lax
from jax.experimental import pallas as pl
from jax.experimental.pallas import tpu as pltpu
from jax.sharding import PartitionSpec as P

BF16 = jnp.bfloat16
F32 = jnp.float32


def iota(shape, dim):
    return lax.broadcasted_iota(jnp.int32, shape, dim)


def ones_where(mask):
    return jnp.where(mask, 1.0, 0.0).astype(BF16)


def mm(a, b):
    return jnp.dot(a, b, preferred_element_type=F32)


def kernel(
    R, G, cap, fgrp,
    idx_ref, tab_hbm, w_hbm, b_ref, wo_ref,
    tg_ref, loss_ref,
    tab, tb, w, col, of, ranked_bf, req_send, req_recv, fet_send, rows, looked,
    p_ref, pt_ref, st_ref, part_f32, part_send, part_recv, gp, rg, g_send, g_recv,
    local_sem, ss0, rs0, ss1, rs1, ss2, rs2, ssp, rsp, ssg, rsg,
):
    me = lax.axis_index("rows")
    mg = lax.axis_index("grp")
    n_rows = tab.shape[1]
    emb = tab.shape[2]
    nl = idx_ref.shape[1]
    per = nl // 3
    bdev = per // fgrp
    share = bdev // G
    r8 = R * 8
    slots = R * cap

    barrier = pltpu.get_barrier_semaphore()

    def up(k):
        return lax.rem(me + k, R)

    def down(k):
        return lax.rem(me - k + R, R)

    def gup(k):
        return lax.rem(mg + k, G)

    @pl.loop(1, R)
    def _(k):
        pl.semaphore_signal(barrier, inc=1, device_id={"rows": up(k)})

    @pl.loop(1, G)
    def _(k):
        pl.semaphore_signal(barrier, inc=1, device_id={"grp": gup(k)})

    tab_copy = pltpu.make_async_copy(tab_hbm, tab, local_sem.at[0])
    w_copy = pltpu.make_async_copy(w_hbm, w, local_sem.at[1])
    tab_copy.start()
    w_copy.start()

    for j in range(nl // 128):
        col[pl.ds(j * 128, 128), :] = idx_ref[:, pl.ds(j * 128, 128)].T
    for t in range(3):
        at = pl.ds(t * per, per)
        of[at, :] = ones_where(iota((per, n_rows), 1) == col[at, 1:2])
    owner_hot = ones_where(iota((r8, nl), 0) == idx_ref[0:1, :])
    present = mm(owner_hot, of[...]) > 0.5
    before = ones_where(iota((n_rows, n_rows), 0) < iota((n_rows, n_rows), 1))
    ranked = jnp.where(present, mm(ones_where(present), before), -1.0)
    ranked_bf[...] = ranked.astype(BF16)
    req_send[...] = ranked.reshape(R, 8, n_rows)

    pl.semaphore_wait(barrier, R - 1 + G - 1)

    def req_copy(k):
        return pltpu.make_async_remote_copy(
            req_send.at[up(k)], req_recv.at[me], ss0.at[k], rs0.at[k],
            device_id={"rows": up(k)}, device_id_type=pl.DeviceIdType.MESH,
        )

    @pl.loop(1, R)
    def _(k):
        req_copy(k).start()

    tab_copy.wait()
    tb[...] = tab[...].astype(BF16)
    req_recv[me] = req_send[me]

    for t in range(3):
        at = pl.ds(t * per, per)
        own_hot = ones_where(iota((per, r8), 1) == col[at, 0:1])
        picked = mm(own_hot, ranked_bf[...]) * of[at, :].astype(F32)
        slot = jnp.sum(picked, axis=1, keepdims=True) + col[at, 3:4].astype(F32)
        looked[t] = jnp.broadcast_to(slot, (per, emb))

    def fetch(src):
        for t in range(3):
            pick = ones_where(
                iota((cap, n_rows), 0).astype(F32) == req_recv[src, pl.ds(t, 1), :]
            )
            fet_send[src, t] = mm(pick, tb[t]).astype(BF16)

    def row_copy(k):
        return pltpu.make_async_remote_copy(
            fet_send.at[down(k)], rows.at[me], ss1.at[k], rs1.at[k],
            device_id={"rows": down(k)}, device_id_type=pl.DeviceIdType.MESH,
        )

    @pl.loop(1, R)
    def _(k):
        req_copy(k).wait_recv()
        fetch(down(k))
        row_copy(k).start()

    fetch(me)
    rows[me] = fet_send[me]

    lane_slot = iota((per, slots), 1).astype(F32)
    for t in range(3):
        slot = looked[t]
        p_ref[t] = ones_where(lane_slot == slot[:, 0:1])
        slot_row = slot.T[0:1, :]
        pt_ref[t] = ones_where(iota((slots, per), 0).astype(F32) == slot_row)
    req_cols = req_recv[...].reshape(r8, n_rows).T.astype(BF16)
    row_i = iota((r8, slots), 0)
    col_j = iota((r8, slots), 1)
    first = (row_i >> 3) * cap
    slot_in = (iota((n_rows, slots), 1) & (cap - 1)).astype(F32)
    for t in range(3):
        spread = ones_where(((row_i & 7) == t) & (col_j >= first) & (col_j < first + cap))
        st_ref[t] = ones_where(mm(req_cols, spread) == slot_in)

    @pl.loop(1, R)
    def _(k):
        row_copy(k).wait_recv()

    for t in range(3):
        looked[t] = mm(p_ref[t], rows[:, t].reshape(slots, emb))
    embedded = (looked[0] * looked[1] + looked[2]).astype(BF16)
    features = jnp.concatenate(
        [embedded[f * bdev : (f + 1) * bdev] for f in range(fgrp)], axis=1
    )
    w_copy.wait()
    partial = mm(features, w[...])
    hidden = partial.shape[1]
    part_f32[...] = partial.reshape(G, share, hidden)
    part_send[...] = partial.astype(BF16).reshape(G, share, hidden)

    def part_copy(k):
        return pltpu.make_async_remote_copy(
            part_send.at[gup(k)], part_recv.at[k], ssp.at[k], rsp.at[k],
            device_id={"grp": gup(k)}, device_id_type=pl.DeviceIdType.MESH,
        )

    for k in range(1, G):
        part_copy(k).start()
    pre = part_f32[mg] + b_ref[...]
    for k in range(1, G):
        part_copy(k).wait_recv()
        pre = pre + part_recv[k].astype(F32)
    sig = jax.nn.sigmoid(pre)
    w_out = wo_ref[...]
    logits = jnp.sum(pre * sig * w_out, axis=1, keepdims=True)
    targets = col[pl.ds(pl.multiple_of(mg * share, share), share), 2:3].astype(F32)
    grad_logit = jax.nn.sigmoid(logits) - targets
    gp[mg] = (grad_logit * w_out * (sig * (1.0 + pre * (1.0 - sig)))).astype(BF16)

    def gp_copy(k):
        return pltpu.make_async_remote_copy(
            gp.at[mg], gp.at[mg], ssg.at[k], rsg.at[k],
            device_id={"grp": gup(k)}, device_id_type=pl.DeviceIdType.MESH,
        )

    for k in range(1, G):
        gp_copy(k).start()
    losses = (
        jnp.maximum(logits, 0.0) + jnp.log1p(jnp.exp(-jnp.abs(logits))) - targets * logits
    )
    diag = iota((share, share), 0) == iota((share, share), 1)
    loss_ref[...] = jnp.sum(jnp.where(diag, losses, 0.0), axis=0, keepdims=True)
    for k in range(1, G):
        gp_copy(k).wait_recv()

    grad_emb = lax.dot_general(
        gp[...].reshape(bdev, hidden), w[...], (((1,), (1,)), ((), ())),
        preferred_element_type=F32,
    )
    grad_rows = jnp.concatenate(
        [grad_emb[:, f * emb : (f + 1) * emb] for f in range(fgrp)], axis=0
    )
    rg[0] = (grad_rows * looked[1]).astype(BF16)
    rg[1] = (grad_rows * looked[0]).astype(BF16)
    rg[2] = grad_rows.astype(BF16)

    def collect(dst):
        for t in range(3):
            hot = pt_ref[t, pl.ds(pl.multiple_of(dst * cap, cap), cap), :]
            g_send[dst, t] = mm(hot, rg[t]).astype(BF16)

    def grad_copy(k):
        return pltpu.make_async_remote_copy(
            g_send.at[up(k)], g_recv.at[me], ss2.at[k], rs2.at[k],
            device_id={"rows": up(k)}, device_id_type=pl.DeviceIdType.MESH,
        )

    @pl.loop(1, R)
    def _(k):
        collect(up(k))
        grad_copy(k).start()

    collect(me)
    g_recv[me] = g_send[me]

    @pl.loop(1, R)
    def _(k):
        req_copy(k).wait_send()
        row_copy(k).wait_send()

    for k in range(1, G):
        part_copy(k).wait_send()
        gp_copy(k).wait_send()

    @pl.loop(1, R)
    def _(k):
        grad_copy(k).wait_recv()

    for t in range(3):
        tg_ref[t] = mm(st_ref[t], g_recv[:, t].reshape(slots, emb))

    @pl.loop(1, R)
    def _(k):
        grad_copy(k).wait_send()


def body(owner, offset, tables, w_first, b_first, w_out, labels):
    R, G = lax.axis_size("rows"), lax.axis_size("grp")
    bdev, fgrp = owner.shape[0], owner.shape[1]
    n_rows, emb = tables.shape[1], tables.shape[2]
    hidden = w_first.shape[1]
    per = bdev * fgrp
    nl = 3 * per
    hot_count = 8 * (per * 7 // (16 * R)) + 8
    cap = 16
    while cap < hot_count // 3:
        cap *= 2
    share = bdev // G
    slots = R * cap

    owner_rows = owner.transpose(2, 1, 0).reshape(1, nl)
    offset_rows = offset.transpose(2, 1, 0).reshape(1, nl)
    kind = jnp.arange(nl, dtype=jnp.int32)[None, :] // per
    label_row = jnp.pad(labels, (0, nl - bdev))[None, :]
    idx = jnp.concatenate(
        [owner_rows * 8 + kind, offset_rows, label_row, owner_rows * cap,
         jnp.zeros((4, nl), jnp.int32)],
        axis=0,
    )
    vmem = pl.BlockSpec(memory_space=pltpu.VMEM)
    hbm = pl.BlockSpec(memory_space=pl.ANY)
    sems = pltpu.SemaphoreType.DMA
    table_grad, losses = pl.pallas_call(
        functools.partial(kernel, R, G, cap, fgrp),
        out_shape=(
            jax.ShapeDtypeStruct((3, n_rows, emb), F32),
            jax.ShapeDtypeStruct((1, share), F32),
        ),
        in_specs=[vmem, hbm, hbm, vmem, vmem],
        out_specs=(vmem, vmem),
        scratch_shapes=[
            pltpu.VMEM((3, n_rows, emb), F32),
            pltpu.VMEM((3, n_rows, emb), BF16),
            pltpu.VMEM(w_first.shape, BF16),
            pltpu.VMEM((nl, 8), jnp.int32),
            pltpu.VMEM((nl, n_rows), BF16),
            pltpu.VMEM((R * 8, n_rows), BF16),
            pltpu.VMEM((R, 8, n_rows), F32),
            pltpu.VMEM((R, 8, n_rows), F32),
            pltpu.VMEM((R, 3, cap, emb), BF16),
            pltpu.VMEM((R, 3, cap, emb), BF16),
            pltpu.VMEM((3, per, emb), F32),
            pltpu.VMEM((3, per, slots), BF16),
            pltpu.VMEM((3, slots, per), BF16),
            pltpu.VMEM((3, n_rows, slots), BF16),
            pltpu.VMEM((G, share, hidden), F32),
            pltpu.VMEM((G, share, hidden), BF16),
            pltpu.VMEM((G, share, hidden), BF16),
            pltpu.VMEM((G, share, hidden), BF16),
            pltpu.VMEM((3, per, emb), BF16),
            pltpu.VMEM((R, 3, cap, emb), BF16),
            pltpu.VMEM((R, 3, cap, emb), BF16),
            sems((2,)),
            sems((R,)), sems((R,)), sems((R,)), sems((R,)), sems((R,)), sems((R,)),
            sems((G,)), sems((G,)), sems((G,)), sems((G,)),
        ],
        compiler_params=pltpu.CompilerParams(
            collective_id=0, has_side_effects=True, vmem_limit_bytes=60 * 1024 * 1024
        ),
        name="embed_step",
    )(idx, tables, w_first, b_first.reshape(1, hidden), w_out.reshape(1, hidden))
    return table_grad, losses.reshape(share)


def solution(mesh):
    placed = (
        P("rows", "grp", None),
        P("rows", "grp", None),
        P("grp", "rows", None),
        P("grp", None),
        P(),
        P(),
        P("rows"),
    )
    return jax.shard_map(
        body,
        mesh=mesh,
        in_specs=placed,
        out_specs=(P("grp", "rows", None), P(("rows", "grp"))),
        check_vma=False,
    )
```

time: 226 us -> 63.7 us (0.28)
  the two profiles are of different devices: /device:TPU:0 before, /device:TPU:13 now
where the time goes in v1:
time: 63.7 us; the launch traced here: 63.4 us
  Pallas kernels  57.2 us (90%)
  local copies, waits for them, and re-layouts  4.72 us (7%)
  other arithmetic  0.73 us (1%)
  between operations  0.67 us (1%)
    pallas_call x1, Pallas kernels, body(): pl.pallas_call(functools.partial(kernel, R, G, cap, fgrp), out_shape=(jax...  57.2 us
    unnamed x4, local copies, waits for them, and re-layouts  2.58 us

profile of v1, /device:TPU:13, one launch (start us, length us, event | category | flops | bytes accessed | tf_op | source)
XLA Modules:
  0.0 63.4 jit_solution(17767194409113748366)
XLA Ops:
  0.6 0.7 %copy.10 = s32[3,6,128]{2,1,0:T(8,128)S(1)} copy(s32[3,6,128]{2,0,1:T(4,128)} %bitcast.8) | data formatting | bytes 18432 | tf_op jit(solution)/shard_map/transpose | solution.py:258
  1.4 0.7 %pad.4 = s32[2304]{0:T(1024)S(1)} pad(s32[128]{0:T(128)} %param.13, s32[]{:T(128)} %constant.14.clone.1), padding=0_2176 | pad | bytes 9732 | tf_op jit(solution)/shard_map/jit(_pad)/pad | solution.py:260
  2.0 0.7 %multiply_bitcast_fusion = (s32[3,6,128]{2,0,1:T(4,128)S(1)}, s32[3,6,128]{2,0,1:T(4,128)S(1)}) fusion(s32[128,6,3]{0,2,1:T(4,128)} %param.7), kind=kLoop, calls=%fused_computation.4 | loop fusion | flops 4608 | bytes 27648 | tf_op jit(solution)/shard_map/mul | solution.py:262
  2.8 0.7 %concatenate.3.idx_ref = s32[8,2304]{1,0:T(8,128)} concatenate(s32[1,2304]{1,0:T(1,128)S(1)} %fusion, s32[1,2304]{1,0:T(1,128)S(1)} %reshape.93, s32[1,2304]{1,0:T(1,128)S(1)} %broadcast_in_dim.7, s32[1,2304]{1,0:T(1,128)S(1)} %mul.47, s32[4,2304]{1,0:T(4,128)S(1)} %broadcast_in_dim.8), dimensions={0} | concatenate | bytes 147456 | tf_op jit(solution)/shard_map/concatenate | solution.py:261
  3.5 57.2 %embed_step.1 = (f32[3,512,128]{2,1,0:T(8,128)}, f32[1,32]{1,0:T(1,128)}) custom-call(s32[8,2304]{1,0:T(8,128)} %concatenate.3.idx_ref, f32[3,512,128]{2,1,0:T(8,128)} %tab_hbm.1, bf16[768,1024]{1,0:T(8,128)(2,1)} %w_hbm.1, f32[1,1024]{1,0:T(1,128)} %bitcast.9, f32[1,1024]{1,0:T(1,128)} %bitcast.10), custom_call_target="tpu_custom_call" | custom-call | tf_op jit(solution)/shard_map/embed_step/pallas_call | solution.py:269
  60.8 0.0 copy-start
  60.8 2.1 %copy.14 = f32[3,512,128]{2,1,0:T(8,128)} copy(f32[3,512,128]{2,1,0:T(8,128)} %get-tuple-element.10) | data formatting | bytes 1572864
  62.9 0.0 copy-done
  62.9 0.5 copy.15
  (8 shorter events, 0.1 us)
Async XLA Ops:
  60.8 2.1 %copy-start = (f32[1,32]{1,0:T(1,128)S(1)}, f32[1,32]{1,0:T(1,128)}, u32[]{:S(2)}) copy-start(f32[1,32]{1,0:T(1,128)} %get-tuple-element.5) | copy-start | bytes 388

commit v2 on v1

--- a/solution.py
+++ b/solution.py
@@ -19,16 +19,29 @@
     return jnp.where(mask, 1.0, 0.0).astype(BF16)
 
 
+def join_bands(bands, starts, width, total):
+    cuts = sorted({0, total, *starts, *(min(s + width, total) for s in starts)})
+    pieces = []
+    for lo, hi in zip(cuts[:-1], cuts[1:]):
+        piece = None
+        for band, s in zip(bands, starts):
+            if s <= lo and hi <= s + width:
+                part = band[lo - s : hi - s]
+                piece = part if piece is None else piece + part
+        pieces.append(piece)
+    return jnp.concatenate(pieces, axis=0).astype(BF16)
+
+
 def mm(a, b):
     return jnp.dot(a, b, preferred_element_type=F32)
 
 
 def kernel(
-    R, G, cap, fgrp,
-    idx_ref, tab_hbm, w_hbm, b_ref, wo_ref,
+    R, G, cap, fgrp, starts, width,
+    own_ref, off_ref, lab_ref, tab_hbm, w_hbm, b_ref, wo_ref,
     tg_ref, loss_ref,
-    tab, tb, w, col, of, ranked_bf, req_send, req_recv, fet_send, rows, looked,
-    p_ref, pt_ref, st_ref, part_f32, part_send, part_recv, gp, rg, g_send, g_recv,
+    idx_ref, tab, tb, w, col, of, ranked_bf, req_send, req_recv, fet_send, rows, looked,
+    p_ref, pt_ref, st_ref, part_f32, part_send, swap_recv, pair_send, pair_recv, gp, rg, g_send, g_recv,
     local_sem, ss0, rs0, ss1, rs1, ss2, rs2, ssp, rsp, ssg, rsg,
 ):
     me = lax.axis_index("rows")
@@ -40,8 +53,10 @@
     bdev = per // fgrp
     share = bdev // G
     r8 = R * 8
-    slots = R * cap
-
+    slots = R * width
+
+    total = fet_send.shape[1]
+    joined = functools.partial(join_bands, starts=starts, width=width, total=total)
     barrier = pltpu.get_barrier_semaphore()
 
     def up(k):
@@ -66,6 +81,15 @@
     tab_copy.start()
     w_copy.start()
 
+    idx_ref[...] = jnp.zeros_like(idx_ref)
+    idx_ref[2:3, 0:bdev] = lab_ref[...]
+    for t in range(3):
+        for f in range(fgrp):
+            lanes = pl.ds(t * per + f * bdev, bdev)
+            owner = own_ref[f, t : t + 1, :]
+            idx_ref[0:1, lanes] = owner * 8 + t
+            idx_ref[1:2, lanes] = off_ref[f, t : t + 1, :]
+            idx_ref[3:4, lanes] = owner * width + (t * (cap // 3) - starts[t])
     for j in range(nl // 128):
         col[pl.ds(j * 128, 128), :] = idx_ref[:, pl.ds(j * 128, 128)].T
     for t in range(3):
@@ -102,11 +126,14 @@
         looked[t] = jnp.broadcast_to(slot, (per, emb))
 
     def fetch(src):
+        rank = req_recv[src]
+        bands = []
         for t in range(3):
-            pick = ones_where(
-                iota((cap, n_rows), 0).astype(F32) == req_recv[src, pl.ds(t, 1), :]
-            )
-            fet_send[src, t] = mm(pick, tb[t]).astype(BF16)
+            shift = t * (cap // 3) - starts[t]
+            line = (iota((width, n_rows), 0) - shift).astype(F32)
+            line = jnp.where(line < 0.0, -2.0, line)
+            bands.append(mm(ones_where(line == rank[t : t + 1, :]), tb[t]))
+        fet_send[src] = joined(bands)
 
     def row_copy(k):
         return pltpu.make_async_remote_copy(
@@ -132,18 +159,20 @@
     req_cols = req_recv[...].reshape(r8, n_rows).T.astype(BF16)
     row_i = iota((r8, slots), 0)
     col_j = iota((r8, slots), 1)
-    first = (row_i >> 3) * cap
-    slot_in = (iota((n_rows, slots), 1) & (cap - 1)).astype(F32)
-    for t in range(3):
-        spread = ones_where(((row_i & 7) == t) & (col_j >= first) & (col_j < first + cap))
-        st_ref[t] = ones_where(mm(req_cols, spread) == slot_in)
+    first = (row_i >> 3) * width
+    slot_in = iota((n_rows, slots), 1) & (width - 1)
+    for t in range(3):
+        spread = ones_where(((row_i & 7) == t) & (col_j >= first) & (col_j < first + width))
+        line = (slot_in - (t * (cap // 3) - starts[t])).astype(F32)
+        line = jnp.where(line < 0.0, -2.0, line)
+        st_ref[t] = ones_where(mm(req_cols, spread) == line)
 
     @pl.loop(1, R)
     def _(k):
         row_copy(k).wait_recv()
 
     for t in range(3):
-        looked[t] = mm(p_ref[t], rows[:, t].reshape(slots, emb))
+        looked[t] = mm(p_ref[t], rows[:, starts[t] : starts[t] + width].reshape(slots, emb))
     embedded = (looked[0] * looked[1] + looked[2]).astype(BF16)
     features = jnp.concatenate(
         [embedded[f * bdev : (f + 1) * bdev] for f in range(fgrp)], axis=1
@@ -151,46 +180,65 @@
     w_copy.wait()
     partial = mm(features, w[...])
     hidden = partial.shape[1]
-    part_f32[...] = partial.reshape(G, share, hidden)
-    part_send[...] = partial.astype(BF16).reshape(G, share, hidden)
+    half = G // 2
+    side = lax.rem(mg, 2)
+    partner = mg + 1 - 2 * side
+    mine = lax.div(mg, 2)
+    for g in range(G):
+        block = partial[g * share : (g + 1) * share]
+        part_f32[g % 2, g // 2] = block
+        part_send[g % 2, g // 2] = block.astype(BF16)
+    swap = pltpu.make_async_remote_copy(
+        part_send.at[1 - side], swap_recv, ssp.at[0], rsp.at[0],
+        device_id={"grp": partner}, device_id_type=pl.DeviceIdType.MESH,
+    )
+    swap.start()
 
     def part_copy(k):
+        peer = lax.rem(mg + 2 * k, G)
         return pltpu.make_async_remote_copy(
-            part_send.at[gup(k)], part_recv.at[k], ssp.at[k], rsp.at[k],
-            device_id={"grp": gup(k)}, device_id_type=pl.DeviceIdType.MESH,
+            pair_send, pair_recv.at[k], ssp.at[k], rsp.at[k],
+            device_id={"grp": peer}, device_id_type=pl.DeviceIdType.MESH,
         )
 
-    for k in range(1, G):
+    swap.wait_recv()
+    pair = part_f32[side] + swap_recv[...].astype(F32)
+    pair_send[...] = pair.astype(BF16)
+    for k in range(1, half):
         part_copy(k).start()
-    pre = part_f32[mg] + b_ref[...]
-    for k in range(1, G):
+    pair = pair + b_ref[...]
+    for k in range(1, half):
         part_copy(k).wait_recv()
-        pre = pre + part_recv[k].astype(F32)
+        pair = pair + pair_recv[k].astype(F32)
+    pre = pair.reshape(half * share, hidden)
     sig = jax.nn.sigmoid(pre)
     w_out = wo_ref[...]
     logits = jnp.sum(pre * sig * w_out, axis=1, keepdims=True)
-    targets = col[pl.ds(pl.multiple_of(mg * share, share), share), 2:3].astype(F32)
+    targets = jnp.concatenate(
+        [
+            col[pl.ds(pl.multiple_of((2 * j + side) * share, share), share), 2:3]
+            for j in range(half)
+        ],
+        axis=0,
+    ).astype(F32)
     grad_logit = jax.nn.sigmoid(logits) - targets
-    gp[mg] = (grad_logit * w_out * (sig * (1.0 + pre * (1.0 - sig)))).astype(BF16)
-
-    def gp_copy(k):
-        return pltpu.make_async_remote_copy(
-            gp.at[mg], gp.at[mg], ssg.at[k], rsg.at[k],
-            device_id={"grp": gup(k)}, device_id_type=pl.DeviceIdType.MESH,
-        )
-
-    for k in range(1, G):
-        gp_copy(k).start()
+    grad_half = (grad_logit * w_out * (sig * (1.0 + pre * (1.0 - sig)))).astype(BF16)
+    gp[side] = grad_half.reshape(half, share, hidden)
+    gp_copy = pltpu.make_async_remote_copy(
+        gp.at[side], gp.at[side], ssg.at[0], rsg.at[0],
+        device_id={"grp": partner}, device_id_type=pl.DeviceIdType.MESH,
+    )
+    gp_copy.start()
     losses = (
         jnp.maximum(logits, 0.0) + jnp.log1p(jnp.exp(-jnp.abs(logits))) - targets * logits
     )
-    diag = iota((share, share), 0) == iota((share, share), 1)
+    diag = iota((half * share, share), 0) - mine * share == iota((half * share, share), 1)
     loss_ref[...] = jnp.sum(jnp.where(diag, losses, 0.0), axis=0, keepdims=True)
-    for k in range(1, G):
-        gp_copy(k).wait_recv()
+    gp_copy.wait_recv()
+    grad_pre = jnp.concatenate([gp[g % 2, g // 2] for g in range(G)], axis=0)
 
     grad_emb = lax.dot_general(
-        gp[...].reshape(bdev, hidden), w[...], (((1,), (1,)), ((), ())),
+        grad_pre, w[...], (((1,), (1,)), ((), ())),
         preferred_element_type=F32,
     )
     grad_rows = jnp.concatenate(
@@ -201,9 +249,8 @@
     rg[2] = grad_rows.astype(BF16)
 
     def collect(dst):
-        for t in range(3):
-            hot = pt_ref[t, pl.ds(pl.multiple_of(dst * cap, cap), cap), :]
-            g_send[dst, t] = mm(hot, rg[t]).astype(BF16)
+        at = pl.ds(pl.multiple_of(dst * width, width), width)
+        g_send[dst] = joined([mm(pt_ref[t, at, :], rg[t]) for t in range(3)])
 
     def grad_copy(k):
         return pltpu.make_async_remote_copy(
@@ -224,16 +271,17 @@
         req_copy(k).wait_send()
         row_copy(k).wait_send()
 
-    for k in range(1, G):
+    swap.wait_send()
+    gp_copy.wait_send()
+    for k in range(1, half):
         part_copy(k).wait_send()
-        gp_copy(k).wait_send()
 
     @pl.loop(1, R)
     def _(k):
         grad_copy(k).wait_recv()
 
     for t in range(3):
-        tg_ref[t] = mm(st_ref[t], g_recv[:, t].reshape(slots, emb))
+        tg_ref[t] = mm(st_ref[t], g_recv[:, starts[t] : starts[t] + width].reshape(slots, emb))
 
     @pl.loop(1, R)
     def _(k):
@@ -248,33 +296,33 @@
     per = bdev * fgrp
     nl = 3 * per
     hot_count = 8 * (per * 7 // (16 * R)) + 8
-    cap = 16
-    while cap < hot_count // 3:
-        cap *= 2
+    uniq = hot_count // 3
+    cap = 3 * uniq
+    total = -(-cap // 16) * 16
+    starts = [t * uniq // 16 * 16 for t in range(3)]
+    width = 16
+    while any(s + width < (t + 1) * uniq for t, s in enumerate(starts)):
+        width *= 2
+    total = max(total, max(starts) + width)
     share = bdev // G
-    slots = R * cap
-
-    owner_rows = owner.transpose(2, 1, 0).reshape(1, nl)
-    offset_rows = offset.transpose(2, 1, 0).reshape(1, nl)
-    kind = jnp.arange(nl, dtype=jnp.int32)[None, :] // per
-    label_row = jnp.pad(labels, (0, nl - bdev))[None, :]
-    idx = jnp.concatenate(
-        [owner_rows * 8 + kind, offset_rows, label_row, owner_rows * cap,
-         jnp.zeros((4, nl), jnp.int32)],
-        axis=0,
-    )
+    half = G // 2
+    slots = R * width
+
+    owner_rows = owner.transpose(1, 2, 0)
+    offset_rows = offset.transpose(1, 2, 0)
     vmem = pl.BlockSpec(memory_space=pltpu.VMEM)
     hbm = pl.BlockSpec(memory_space=pl.ANY)
     sems = pltpu.SemaphoreType.DMA
     table_grad, losses = pl.pallas_call(
-        functools.partial(kernel, R, G, cap, fgrp),
+        functools.partial(kernel, R, G, cap, fgrp, starts, width),
         out_shape=(
             jax.ShapeDtypeStruct((3, n_rows, emb), F32),
             jax.ShapeDtypeStruct((1, share), F32),
         ),
-        in_specs=[vmem, hbm, hbm, vmem, vmem],
+        in_specs=[vmem, vmem, vmem, hbm, hbm, vmem, vmem],
         out_specs=(vmem, vmem),
         scratch_shapes=[
+            pltpu.VMEM((8, nl), jnp.int32),
             pltpu.VMEM((3, n_rows, emb), F32),
             pltpu.VMEM((3, n_rows, emb), BF16),
             pltpu.VMEM(w_first.shape, BF16),
@@ -283,19 +331,21 @@
             pltpu.VMEM((R * 8, n_rows), BF16),
             pltpu.VMEM((R, 8, n_rows), F32),
             pltpu.VMEM((R, 8, n_rows), F32),
-            pltpu.VMEM((R, 3, cap, emb), BF16),
-            pltpu.VMEM((R, 3, cap, emb), BF16),
+            pltpu.VMEM((R, total, emb), BF16),
+            pltpu.VMEM((R, total, emb), BF16),
             pltpu.VMEM((3, per, emb), F32),
             pltpu.VMEM((3, per, slots), BF16),
             pltpu.VMEM((3, slots, per), BF16),
             pltpu.VMEM((3, n_rows, slots), BF16),
-            pltpu.VMEM((G, share, hidden), F32),
-            pltpu.VMEM((G, share, hidden), BF16),
-            pltpu.VMEM((G, share, hidden), BF16),
-            pltpu.VMEM((G, share, hidden), BF16),
+            pltpu.VMEM((2, half, share, hidden), F32),
+            pltpu.VMEM((2, half, share, hidden), BF16),
+            pltpu.VMEM((half, share, hidden), BF16),
+            pltpu.VMEM((half, share, hidden), BF16),
+            pltpu.VMEM((half, half, share, hidden), BF16),
+            pltpu.VMEM((2, half, share, hidden), BF16),
             pltpu.VMEM((3, per, emb), BF16),
-            pltpu.VMEM((R, 3, cap, emb), BF16),
-            pltpu.VMEM((R, 3, cap, emb), BF16),
+            pltpu.VMEM((R, total, emb), BF16),
+            pltpu.VMEM((R, total, emb), BF16),
             sems((2,)),
             sems((R,)), sems((R,)), sems((R,)), sems((R,)), sems((R,)), sems((R,)),
             sems((G,)), sems((G,)), sems((G,)), sems((G,)),
@@ -304,7 +354,7 @@
             collective_id=0, has_side_effects=True, vmem_limit_bytes=60 * 1024 * 1024
         ),
         name="embed_step",
-    )(idx, tables, w_first, b_first.reshape(1, hidden), w_out.reshape(1, hidden))
+    )(owner_rows, offset_rows, labels.reshape(1, bdev), tables, w_first, b_first.reshape(1, hidden), w_out.reshape(1, hidden))
     return table_grad, losses.reshape(share)
 
 

time: 63.7 us -> 57.2 us (0.90)
  Pallas kernels: 57.2 us -> 53.7 us
  local copies, waits for them, and re-layouts: 4.72 us -> 2.58 us
  other arithmetic: 0.73 us -> 0 us
    pallas_call x1, Pallas kernels: 57.2 us -> 53.7 us  [body(): pl.pallas_call(functools.partial(kernel, R, G, cap, fgrp, starts, width),...]
    mul x1 -> x0, other arithmetic: 0.71 us -> none  [body(): owner_rows * cap]
    transpose x1 -> x0, local copies, waits for them, and re-layouts: 0.71 us -> none  [body(): offset_rows = offset.transpose(2, 1, 0).reshape(1, nl)]
    concatenate x1 -> x0, local copies, waits for them, and re-layouts: 0.7 us -> none  [body(): jnp.concatenate([owner_rows * 8 + kind, offset_rows, label_row, owner_row...]
    pad x1 -> x0, local copies, waits for them, and re-layouts: 0.66 us -> none  [body(): label_row = jnp.pad(labels, (0, nl - bdev))[None, :]]
where the time goes in v2:
time: 57.2 us; the launch traced here: 57 us
  Pallas kernels  53.7 us (94%)
  local copies, waits for them, and re-layouts  2.58 us (5%)
  between operations  0.65 us (1%)
    pallas_call x1, Pallas kernels, body(): pl.pallas_call(functools.partial(kernel, R, G, cap, fgrp, starts, width),...  53.7 us
    unnamed x4, local copies, waits for them, and re-layouts  2.58 us

profile of v2, /device:TPU:13, one launch (start us, length us, event | category | flops | bytes accessed | tf_op | source)
XLA Modules:
  0.0 57.0 jit_solution(14182422313117472176)
XLA Ops:
  0.6 53.7 %embed_step.1 = (f32[3,512,128]{2,1,0:T(8,128)}, f32[1,32]{1,0:T(1,128)}) custom-call(s32[6,3,128]{2,1,0:T(4,128)} %bitcast.6, s32[6,3,128]{2,1,0:T(4,128)} %bitcast.7, s32[1,128]{1,0:T(1,128)} %bitcast.10, f32[3,512,128]{2,1,0:T(8,128)} %tab_hbm.1, bf16[768,1024]{1,0:T(8,128)(2,1)} %w_hbm.1, f32[1,1024]{1,0:T(1,128)} %bitcast.8, f32[1,1024]{1,0:T(1,128)} %bitcast.9), custom_call_target="tpu_custom_call" | custom-call | tf_op jit(solution)/shard_map/embed_step/pallas_call | solution.py:316
  54.4 0.0 copy-start
  54.4 2.1 %copy.11 = f32[3,512,128]{2,1,0:T(8,128)} copy(f32[3,512,128]{2,1,0:T(8,128)} %get-tuple-element.8) | data formatting | bytes 1572864
  56.4 0.0 copy-done
  56.4 0.5 copy.12
Async XLA Ops:
  54.4 2.1 %copy-start = (f32[1,32]{1,0:T(1,128)S(1)}, f32[1,32]{1,0:T(1,128)}, u32[]{:S(2)}) copy-start(f32[1,32]{1,0:T(1,128)} %get-tuple-element.5) | copy-start | bytes 388
